TPU v7x, 32 devices: a whole 2x2x4 slice. The times are simulated.
32 devices in a mesh: sp: 16 (over z, y, x), tp: 2 (over core).
Axes of the slice: x: 2, y: 2, z: 4, core: 2. Of those that a mesh axis runs over, the one named last changes fastest.
Arguments:
- fade_rate: float32 [1, 16384, 4096], P(None, 'sp', 'tp'), may hold values from 0.2 to 2
- update_in: bfloat16 [1, 16384, 4096], P(None, 'sp', 'tp'), may hold values from -6 to 6
- norm_gain: float32 [4096], P('tp'), may hold values from 0.25 to 1.75
Outputs:
- mixed_out: bfloat16 [1, 16384, 4096], P(None, 'sp', 'tp')
All inputs are finite; a program needn't handle non-finite values.
Results may differ from a plain program's by a relative error of at most 0.0011.
Values sent between devices are 32-bit elements; how exact they have to be, the bound alone decides.
A program may use at most 128 MiB of HBM per device.

v0:
```python
import jax
import jax.numpy as jnp
from jax import lax
from jax.sharding import PartitionSpec as P


def prefix(part, axis, combine, identity):
    place = lax.axis_index(axis)
    gathered = jax.tree.map(lambda a: lax.all_gather(a, axis), part)
    state = jax.tree.map(lambda a, e: jnp.zeros_like(a) + jnp.asarray(e, a.dtype), part, identity)

    def one(turn, state):
        return combine(
            state, jax.tree.map(lambda a: lax.dynamic_index_in_dim(a, turn, 0, False), gathered)
        )

    return lax.fori_loop(0, place, one, state)


def join_pair(earlier, later):
    return (earlier[0] * later[0], later[0] * earlier[1] + later[1])


def per_device(fade_rate, update_in, norm_gain):
    total_length = fade_rate.shape[1] * lax.axis_size("sp")
    keep = jnp.exp(-fade_rate / total_length)
    push = update_in.astype(jnp.float32) * total_length ** (-0.5)
    steps = -fade_rate / total_length
    logs = jnp.sum(steps, axis=1, keepdims=True) - jnp.cumsum(steps, axis=1)
    summary = (jnp.exp(jnp.sum(steps, axis=1)), jnp.sum(jnp.exp(logs) * push, axis=1))
    entering_forward = prefix(
        summary, "sp", join_pair, (jnp.ones_like(keep[:, 0]), jnp.zeros_like(push[:, 0]))
    )
    started = push.at[:, 0].add(keep[:, 0] * entering_forward[1])
    forward = lax.associative_scan(join_pair, (keep, started), axis=1)[1]
    power = lax.psum(jnp.sum(forward * forward, axis=-1, keepdims=True), "tp") / (
        forward.shape[-1] * lax.axis_size("tp")
    )
    mixed_out = (forward * lax.rsqrt(power + 1e-06) * norm_gain).astype(jnp.bfloat16)
    return mixed_out


def solution(mesh):
    placed = (P(None, "sp", "tp"), P(None, "sp", "tp"), P("tp"))
    return jax.shard_map(
        per_device, mesh=mesh, in_specs=placed, out_specs=P(None, "sp", "tp"), check_vma=False
    )
```

profile of v0, /device:TPU:0, one launch (start us, length us, event | category | flops | bytes accessed | tf_op | source)
XLA Modules:
  0.0 499.0 jit_solution(14313204583995138267)
XLA Ops:
  0.0 11.9 %fusion.20 = (f32[1,1024,2048]{2,1,0:T(8,128)}, f32[2048]{0:T(1024)S(1)}, f32[1,1024,2048]{2,1,0:T(8,128)}) fusion(f32[1,1024,2048]{2,1,0:T(8,128)} %param.7), kind=kLoop, calls=%fused_computation.64 | loop fusion | flops 6289408 | bytes 25174016 | tf_op jit(solution)/shard_map/exp | solution.py:26
  11.9 11.5 %fusion.3 = f32[1,2048,8,128]{1,2,3,0:T(8,128)} fusion(f32[1,2048,8,128]{1,3,2,0:T(8,128)} %bitcast.47), kind=kOutput, calls=%fused_computation.7 | output fusion | flops 266338304 | bytes 16777216 | tf_op jit(solution)/shard_map/reduce-window
  23.4 0.8 slice_bitcast_fusion.1
  24.2 11.4 %copy.8 = f32[1,2048,8,128]{1,3,2,0:T(8,128)} copy(f32[1,2048,8,128]{1,2,3,0:T(8,128)} %fusion.3) | data formatting | bytes 16777216 | tf_op jit(solution)/shard_map/reduce-window
  35.8 8.1 %fusion = (f32[2048]{0:T(1024)S(1)}, f32[1,1024,2048]{2,1,0:T(8,128)}) fusion(f32[1,2048,8,128]{1,3,2,0:T(8,128)} %copy.8, f32[2048,8]{0,1:T(8,128)S(1)} %slice_bitcast_fusion, f32[2048]{0:T(1024)S(1)} %get-tuple-element.75, bf16[1,1024,2048]{2,1,0:T(8,128)(2,1)} %param.8), kind=kLoop, calls=%fused_computation.3 | loop fusion | flops 12580864 | bytes 21053440 | tf_op jit(solution)/shard_map/reduce_sum | solution.py:30
  43.8 43.1 %all-gather.1 = f32[32768]{0:T(1024)S(1)} all-gather(f32[2048]{0:T(1024)S(1)} %get-tuple-element.79), channel_id=3, replica_groups=mesh['sp'=16,'tp'=2] {'sp'}, dimensions={0}, use_global_device_ids=true | all-gather | bytes 139264 | tf_op jit(solution)/shard_map/all_gather | solution.py:9
  86.9 36.1 %all-gather = f32[32768]{0:T(1024)S(1)} all-gather(f32[2048]{0:T(1024)S(1)} %exp.25), channel_id=2, replica_groups=mesh['sp'=16,'tp'=2] {'sp'}, dimensions={0}, use_global_device_ids=true | all-gather | bytes 139264 | tf_op jit(solution)/shard_map/all_gather | solution.py:9
  123.1 0.9 fusion.18
  124.0 1.5 scatter-add.4
  125.5 19.0 %slice.337 = f32[1,511,2048]{2,1,0:T(8,128)} slice(f32[1,1024,2048]{2,1,0:T(8,128)} %scatter-add.4), slice={[0:1:1], [2:1024:2], [0:2048:1]} | slice | bytes 8372224 | tf_op jit(solution)/shard_map/slice | solution.py:35
  144.4 18.5 %slice.267 = f32[1,512,2048]{2,1,0:T(8,128)} slice(f32[1,1024,2048]{2,1,0:T(8,128)} %scatter-add.4), slice={[0:1:1], [1:1024:2], [0:2048:1]} | slice | bytes 8388608 | tf_op jit(solution)/shard_map/slice | solution.py:35
  163.0 18.6 %slice.266 = f32[1,512,2048]{2,1,0:T(8,128)} slice(f32[1,1024,2048]{2,1,0:T(8,128)} %scatter-add.4), slice={[0:1:1], [0:1023:2], [0:2048:1]} | slice | bytes 8388608 | tf_op jit(solution)/shard_map/slice | solution.py:35
  181.6 18.5 %slice.269 = f32[1,512,2048]{2,1,0:T(8,128)} slice(f32[1,1024,2048]{2,1,0:T(8,128)} %get-tuple-element.74), slice={[0:1:1], [0:1023:2], [0:2048:1]} | slice | bytes 8388608 | tf_op jit(solution)/shard_map/slice | solution.py:35
  200.1 18.6 %slice.265 = f32[1,512,2048]{2,1,0:T(8,128)} slice(f32[1,1024,2048]{2,1,0:T(8,128)} %get-tuple-element.74), slice={[0:1:1], [1:1024:2], [0:2048:1]} | slice | bytes 8388608 | tf_op jit(solution)/shard_map/slice | solution.py:35
  218.6 11.9 %fusion.21 = (f32[1,512,2048]{2,1,0:T(8,128)}, f32[1,512,2048]{2,1,0:T(8,128)}) fusion(f32[1,512,2048]{2,1,0:T(8,128)} %slice.269, f32[1,512,2048]{2,1,0:T(8,128)} %slice.265, f32[1,512,2048]{2,1,0:T(8,128)} %slice.267, f32[1,512,2048]{2,1,0:T(8,128)} %slice.266), kind=kLoop, calls=%fused_computation.65 | loop fusion | flops 3145728 | bytes 25165824 | tf_op jit(solution)/shard_map/mul | solution.py:21
  230.5 19.0 %slice.264 = f32[1,511,2048]{2,1,0:T(8,128)} slice(f32[1,1024,2048]{2,1,0:T(8,128)} %get-tuple-element.74), slice={[0:1:1], [2:1024:2], [0:2048:1]} | slice | bytes 8372224 | tf_op jit(solution)/shard_map/slice | solution.py:35
  249.5 0.8 slice.342
  250.3 9.8 %slice.275 = f32[1,256,2048]{2,1,0:T(8,128)} slice(f32[1,512,2048]{2,1,0:T(8,128)} %get-tuple-element.77), slice={[0:1:1], [0:511:2], [0:2048:1]} | slice | bytes 4194304 | tf_op jit(solution)/shard_map/slice | solution.py:35
  260.2 9.8 %slice.271 = f32[1,256,2048]{2,1,0:T(8,128)} slice(f32[1,512,2048]{2,1,0:T(8,128)} %get-tuple-element.77), slice={[0:1:1], [1:512:2], [0:2048:1]} | slice | bytes 4194304 | tf_op jit(solution)/shard_map/slice | solution.py:35
  270.0 10.0 %slice.270 = f32[1,255,2048]{2,1,0:T(8,128)} slice(f32[1,512,2048]{2,1,0:T(8,128)} %get-tuple-element.77), slice={[0:1:1], [2:512:2], [0:2048:1]} | slice | bytes 4177920 | tf_op jit(solution)/shard_map/slice | solution.py:35
  280.0 10.1 %slice.335 = f32[1,255,2048]{2,1,0:T(8,128)} slice(f32[1,512,2048]{2,1,0:T(8,128)} %get-tuple-element.78), slice={[0:1:1], [2:512:2], [0:2048:1]} | slice | bytes 4177920 | tf_op jit(solution)/shard_map/slice | solution.py:35
  290.0 9.8 %slice.273 = f32[1,256,2048]{2,1,0:T(8,128)} slice(f32[1,512,2048]{2,1,0:T(8,128)} %get-tuple-element.78), slice={[0:1:1], [1:512:2], [0:2048:1]} | slice | bytes 4194304 | tf_op jit(solution)/shard_map/slice | solution.py:35
  299.8 9.8 %slice.272 = f32[1,256,2048]{2,1,0:T(8,128)} slice(f32[1,512,2048]{2,1,0:T(8,128)} %get-tuple-element.78), slice={[0:1:1], [0:511:2], [0:2048:1]} | slice | bytes 4194304 | tf_op jit(solution)/shard_map/slice | solution.py:35
  309.7 5.8 %fusion.22 = (f32[1,256,2048]{2,1,0:T(8,128)}, f32[1,256,2048]{2,1,0:T(8,128)S(1)}) fusion(f32[1,256,2048]{2,1,0:T(8,128)} %slice.275, f32[1,256,2048]{2,1,0:T(8,128)} %slice.271, f32[1,256,2048]{2,1,0:T(8,128)} %slice.273, f32[1,256,2048]{2,1,0:T(8,128)} %slice.272), kind=kLoop, calls=%fused_computation.66 | loop fusion | flops 1572864 | bytes 12582912 | tf_op jit(solution)/shard_map/mul | solution.py:21
  315.5 5.4 %slice.281 = f32[1,128,2048]{2,1,0:T(8,128)} slice(f32[1,256,2048]{2,1,0:T(8,128)} %get-tuple-element.81), slice={[0:1:1], [0:255:2], [0:2048:1]} | slice | bytes 2097152 | tf_op jit(solution)/shard_map/slice | solution.py:35
  320.9 5.4 %slice.277 = f32[1,128,2048]{2,1,0:T(8,128)} slice(f32[1,256,2048]{2,1,0:T(8,128)} %get-tuple-element.81), slice={[0:1:1], [1:256:2], [0:2048:1]} | slice | bytes 2097152 | tf_op jit(solution)/shard_map/slice | solution.py:35
  326.3 4.2 slice.276
  330.5 3.0 slice.333
  333.5 2.9 slice.279
  336.3 2.9 slice.278
  339.2 2.5 fusion.23
  341.7 1.5 slice.287
  343.2 1.5 slice.283
  344.6 1.6 slice.282
  346.2 0.4 slice.331
  346.5 0.3 slice.285
  346.8 1.5 slice.284
  348.3 1.5 fusion.24
  349.8 0.1 slice.293
  349.9 0.1 slice.289
  350.1 0.2 slice.288
  350.3 0.2 slice.329
  350.7 0.8 slice.290
  351.5 1.0 fusion.25
  354.6 0.9 add.177
  355.6 2.1 pad.76
  357.7 1.5 fusion.7
  359.4 1.1 pad_maximum_fusion.2
  360.5 4.2 pad.77
  364.7 4.8 pad.78
  369.5 3.8 fusion.6
  373.3 1.6 add.181
  374.9 1.6 pad_maximum_fusion.1
  376.6 16.6 %pad.79 = f32[1,512,2048]{2,1,0:T(8,128)} pad(f32[1,256,2048]{2,1,0:T(8,128)} %pad_maximum_fusion.1, f32[]{:T(128)} %constant.59.clone.1), padding=0_0_0x0_1_1x0_0_0 | pad | bytes 6291460 | tf_op jit(solution)/shard_map/pad | solution.py:35
  393.2 9.0 %pad.80 = f32[1,512,2048]{2,1,0:T(8,128)} pad(f32[1,256,2048]{2,1,0:T(8,128)S(1)} %copy-done.3, f32[]{:T(128)} %constant.59.clone.1), padding=0_0_0x1_0_1x0_0_0 | pad | bytes 6291460 | tf_op jit(solution)/shard_map/pad | solution.py:35
  402.2 7.9 %fusion.5 = f32[1,511,2048]{2,1,0:T(8,128)S(1)} fusion(f32[1,511,2048]{2,1,0:T(8,128)} %slice.337, f32[1,511,2048]{2,1,0:T(8,128)} %slice.264, f32[1,512,2048]{2,1,0:T(8,128)} %pad.80, f32[1,512,2048]{2,1,0:T(8,128)} %pad.79), kind=kLoop, calls=%fused_computation.14 | loop fusion | flops 3139584 | bytes 20930560 | tf_op jit(solution)/shard_map/add | solution.py:21
  410.2 0.3 copy-done.1
  410.5 2.7 add.183
  413.2 2.5 pad_maximum_fusion
  415.7 32.4 %pad.81 = f32[1,1024,2048]{2,1,0:T(8,128)} pad(f32[1,512,2048]{2,1,0:T(8,128)} %pad_maximum_fusion, f32[]{:T(128)} %constant.59.clone.1), padding=0_0_0x0_1_1x0_0_0 | pad | bytes 12582916 | tf_op jit(solution)/shard_map/pad | solution.py:35
  448.1 32.3 %pad.82 = f32[1,1024,2048]{2,1,0:T(8,128)} pad(f32[1,512,2048]{2,1,0:T(8,128)} %add.183, f32[]{:T(128)} %constant.59.clone.1), padding=0_0_0x1_0_1x0_0_0 | pad | bytes 12582916 | tf_op jit(solution)/shard_map/pad | solution.py:35
  480.4 9.9 %multiply_reduce_fusion = (f32[1024]{0:T(1024)S(1)}, f32[1,1024,2048]{2,1,0:T(8,128)}) fusion(f32[1,1024,2048]{2,1,0:T(8,128)} %pad.81, f32[1,1024,2048]{2,1,0:T(8,128)} %pad.82), kind=kLoop, calls=%fused_computation.10 | loop fusion | flops 6290432 | bytes 25169920 | tf_op jit(solution)/shard_map/reduce_sum | solution.py:36
  490.3 2.4 psum.7
  492.8 6.2 %multiply_convert_fusion = bf16[1,1024,2048]{2,1,0:T(8,128)(2,1)} fusion(f32[1,1024,2048]{2,1,0:T(8,128)} %get-tuple-element.73, f32[2048]{0:T(1024)S(1)} %copy-done.5, f32[1024]{0:T(1024)S(1)} %bitcast.50), kind=kLoop, calls=%fused_computation.9 | loop fusion | flops 6291456 | bytes 12595200 | tf_op jit(solution)/shard_map/convert_element_type | solution.py:39
  (80 shorter events, 2.3 us)
Async XLA Ops:
  353.3 1.1 copy-start.4
  369.5 3.8 copy-start.2
  376.6 16.6 %copy-start.3 = (f32[1,256,2048]{2,1,0:T(8,128)S(1)}, f32[1,256,2048]{2,1,0:T(8,128)}, u32[]{:S(2)}) copy-start(f32[1,256,2048]{2,1,0:T(8,128)} %add.181) | copy-start | bytes 6291460
  402.2 8.0 %copy-start = (f32[1,512,2048]{2,1,0:T(8,128)S(1)}, f32[1,512,2048]{2,1,0:T(8,128)}, u32[]{:S(2)}) copy-start(f32[1,512,2048]{2,1,0:T(8,128)} %pad.79) | copy-start | bytes 12582916
  402.2 8.3 %copy-start.1 = (f32[1,512,2048]{2,1,0:T(8,128)S(1)}, f32[1,512,2048]{2,1,0:T(8,128)}, u32[]{:S(2)}) copy-start(f32[1,512,2048]{2,1,0:T(8,128)} %pad.80) | copy-start | bytes 12582916
  480.4 12.4 %copy-start.5 = (f32[2048]{0:T(1024)S(1)}, f32[2048]{0:T(1024)}, u32[]{:S(2)}) copy-start(f32[2048]{0:T(1024)} %param.9) | copy-start | bytes 24580
where the time goes:
time: 505 us; the launch traced here: 499 us
  local copies, waits for them, and re-layouts  321 us (64%)
  other arithmetic  95.5 us (19%)
  blocking collectives  81.7 us (16%)
    slice x59, local copies, waits for them, and re-layouts, per_device(): forward = lax.associative_scan(join_pair, (keep, started), axis=1)[1]  205 us
    pad x18, local copies, waits for them, and re-layouts, per_device(): forward = lax.associative_scan(join_pair, (keep, started), axis=1)[1]  102 us
    all_gather x2, blocking collectives, prefix(): gathered = jax.tree.map(lambda a: lax.all_gather(a, axis), part)  79.2 us
    mul x8, other arithmetic, join_pair(): return (earlier[0] * later[0], later[0] * earlier[1] + later[1])  22.6 us
    add x9, other arithmetic, join_pair(): return (earlier[0] * later[0], later[0] * earlier[1] + later[1])  13.5 us
    another operation x3, local copies, waits for them, and re-layouts  12.3 us
    exp x1, other arithmetic, per_device(): keep = jnp.exp(-fade_rate / total_length)  11.9 us
    another operation x2, other arithmetic  11.5 us

commit v1 on v0

v1 whole, which is shorter than its diff:
```python
import functools

import jax
import jax.numpy as jnp
from jax import lax
from jax.experimental import pallas as pl
from jax.experimental.pallas import tpu as pltpu
from jax.sharding import PartitionSpec as P

MESH = pl.DeviceIdType.MESH
EPS = 1e-06


def piece_of(size, most):
    while size % most:
        most //= 2
    return most


def scan_kernel(
    n, m, length, channels, wide, rows,
    fade_hbm, update_hbm, state_ref, gain_ref,
    fade_buf, update_buf, fall_buf, tri, summary, got, squares, got_squares,
    fade_sem, update_sem, send_sem, recv_sem, sq_send_sem, sq_recv_sem,
):
    me, part = lax.axis_index("sp"), lax.axis_index("tp")
    blocks, span, _ = state_ref.shape
    pieces = span // rows

    def fetch(b):
        columns = pl.ds(pl.multiple_of(b * wide, wide), wide)
        return (
            pltpu.make_async_copy(fade_hbm.at[0, :, columns], fade_buf.at[b], fade_sem.at[b]),
            pltpu.make_async_copy(update_hbm.at[0, :, columns], update_buf.at[b], update_sem.at[b]),
        )

    ahead = min(3, blocks)
    for b in range(ahead):
        for copy in fetch(b):
            copy.start()

    barrier = pltpu.get_barrier_semaphore()

    @pl.loop(1, n)
    def _(step):
        other = lax.rem(me + step, n)
        pl.semaphore_signal(barrier, inc=1, device_id=(other, part), device_id_type=MESH)

    for step in range(1, m):
        other = lax.rem(part + step, m)
        pl.semaphore_signal(barrier, inc=1, device_id=(me, other), device_id_type=MESH)

    later = lax.broadcasted_iota(jnp.int32, (rows, rows), 0)
    sooner = lax.broadcasted_iota(jnp.int32, (rows, rows), 1)
    tri[...] = jnp.where(sooner <= later, 1.0, 0.0).astype(jnp.bfloat16)
    pl.semaphore_wait(barrier, n - 1 + m - 1)

    def tell(b, other):
        return pltpu.make_async_remote_copy(
            src_ref=summary.at[b],
            dst_ref=got.at[me, b],
            send_sem=send_sem.at[b, other],
            recv_sem=recv_sem.at[b, me],
            device_id=(other, part),
            device_id_type=MESH,
        )

    def dot(a, b):
        return jnp.dot(a, b, preferred_element_type=jnp.float32)

    @pl.loop(0, blocks)
    def _(b):
        for copy in fetch(b):
            copy.wait()

        @pl.when(b + ahead < blocks)
        def _():
            for copy in fetch(b + ahead):
                copy.start()

        total_fall = jnp.ones((1, wide), jnp.float32)
        total = jnp.zeros((1, wide), jnp.float32)
        for k in range(pieces):
            here = pl.ds(k * rows, rows)
            fade = fade_buf[b, here, :]
            coarse = fade.astype(jnp.bfloat16)
            fine = (fade - coarse.astype(jnp.float32)).astype(jnp.bfloat16)
            faded = dot(tri[...], coarse) + dot(tri[...], fine)
            push = update_buf[b, here, :]
            growth = jnp.exp(faded * (1.0 / length))
            extra = (push.astype(jnp.float32) * (growth - 1.0)).astype(jnp.bfloat16)
            grown = dot(tri[...], push) + dot(tri[...], extra)
            fall = jnp.exp(faded * (-1.0 / length))
            fall_buf[b, here, :] = fall
            state_ref[b, here, :] = grown
            last_fall = fall[rows - 1 : rows, :]
            total = last_fall * (grown[rows - 1 : rows, :] + total)
            total_fall = total_fall * last_fall
        summary[b, 0:1, :] = total_fall
        summary[b, 1:2, :] = total

        @pl.loop(me + 1, n)
        def _(other):
            tell(b, other).start()

    def take(other, state):
        fresh = []
        for b in range(blocks):
            pltpu.make_async_remote_copy(
                src_ref=summary.at[b],
                dst_ref=got.at[other, b],
                send_sem=send_sem.at[b, other],
                recv_sem=recv_sem.at[b, other],
                device_id=(other, part),
                device_id_type=MESH,
            ).wait_recv()
            fresh.append(got[other, b, 0:1, :] * state[b] + got[other, b, 1:2, :])
        return tuple(fresh)

    entering = lax.fori_loop(
        0, me, take, tuple(jnp.zeros((1, wide), jnp.float32) for _ in range(blocks))
    )

    def share(k, step):
        other = lax.rem(part + step, m)
        return pltpu.make_async_remote_copy(
            src_ref=squares.at[k],
            dst_ref=got_squares.at[step - 1, k],
            send_sem=sq_send_sem.at[step - 1, k],
            recv_sem=sq_recv_sem.at[step - 1, k],
            device_id=(me, other),
            device_id_type=MESH,
        )

    def finish(k, entering):
        here = pl.ds(pl.multiple_of(k * rows, rows), rows)
        square = jnp.zeros((rows, 128), jnp.float32)
        leaving = []
        for b in range(blocks):
            state = fall_buf[b, here, :] * (state_ref[b, here, :] + entering[b])
            state_ref[b, here, :] = state
            for c in range(wide // 128):
                part_state = state[:, c * 128 : (c + 1) * 128]
                square = square + part_state * part_state
            leaving.append(state[rows - 1 : rows, :])
        squares[k] = square
        for step in range(1, m):
            share(k, step).start()
        return tuple(leaving)

    lax.fori_loop(0, pieces, finish, entering)

    @pl.loop(0, pieces)
    def _(k):
        square = squares[k]
        for step in range(1, m):
            share(k, step).wait_recv()
            square = square + got_squares[step - 1, k]
        power = jnp.sum(square, axis=1, keepdims=True) / (length * channels)
        gain = lax.rsqrt(power + EPS) * length ** (-0.5)
        here = pl.ds(pl.multiple_of(k * rows, rows), rows)
        gain_ref[here, :] = jnp.broadcast_to(gain, (rows, 128))

    @pl.loop(0, pieces)
    def _(k):
        for step in range(1, m):
            share(k, step).wait_send()

    @pl.loop(me + 1, n)
    def _(other):
        for b in range(blocks):
            tell(b, other).wait_send()


def norm_kernel(rows, state_ref, gain_ref, norm_gain_ref, out_hbm, out_buf, sem):
    blocks, span, wide = state_ref.shape
    pieces = span // rows

    def put(k):
        here = pl.ds(pl.multiple_of(k * rows, rows), rows)
        return pltpu.make_async_copy(out_buf.at[k], out_hbm.at[0, here, :], sem.at[k])

    @pl.loop(0, pieces)
    def _(k):
        here = pl.ds(pl.multiple_of(k * rows, rows), rows)
        gain = gain_ref[here, :]
        for b in range(blocks):
            for c in range(wide // 128):
                columns = pl.ds(b * wide + c * 128, 128)
                state = state_ref[b, here, pl.ds(c * 128, 128)]
                out_buf[k, :, columns] = (state * gain * norm_gain_ref[:, columns]).astype(
                    out_buf.dtype
                )
        put(k).start()

    @pl.loop(0, pieces)
    def _(k):
        put(k).wait()


def per_device(n, m, fade_rate, update_in, norm_gain):
    _, span, own = fade_rate.shape
    length, channels = span * n, own * m
    wide, rows = piece_of(own, 256), piece_of(span, 128)
    blocks, pieces = own // wide, span // rows
    f32, bf16 = jnp.float32, jnp.bfloat16
    anywhere = pl.BlockSpec(memory_space=pl.ANY)
    in_vmem = pl.BlockSpec(memory_space=pltpu.VMEM)
    dma = pltpu.SemaphoreType.DMA
    state, gain = pl.pallas_call(
        functools.partial(scan_kernel, n, m, length, channels, wide, rows),
        out_shape=(
            pltpu.VMEM((blocks, span, wide), f32),
            pltpu.VMEM((span, 128), f32),
        ),
        in_specs=[anywhere, anywhere],
        out_specs=(in_vmem, in_vmem),
        scratch_shapes=[
            pltpu.VMEM((blocks, span, wide), f32),
            pltpu.VMEM((blocks, span, wide), bf16),
            pltpu.VMEM((blocks, span, wide), f32),
            pltpu.VMEM((rows, rows), bf16),
            pltpu.VMEM((blocks, 2, wide), f32),
            pltpu.VMEM((n, blocks, 2, wide), f32),
            pltpu.VMEM((pieces, rows, 128), f32),
            pltpu.VMEM((m - 1, pieces, rows, 128), f32),
            dma((blocks,)),
            dma((blocks,)),
            dma((blocks, n)),
            dma((blocks, n)),
            dma((m - 1, pieces)),
            dma((m - 1, pieces)),
        ],
        compiler_params=pltpu.CompilerParams(
            collective_id=0, has_side_effects=True, vmem_limit_bytes=44 * 2**20
        ),
        name="scan",
    )(fade_rate, update_in)
    return pl.pallas_call(
        functools.partial(norm_kernel, rows),
        out_shape=jax.ShapeDtypeStruct((1, span, own), bf16),
        in_specs=[in_vmem, in_vmem, in_vmem],
        out_specs=anywhere,
        scratch_shapes=[pltpu.VMEM((pieces, rows, own), bf16), dma((pieces,))],
        compiler_params=pltpu.CompilerParams(vmem_limit_bytes=24 * 2**20),
        name="norm",
    )(state, gain, norm_gain.reshape(1, own))


def solution(mesh):
    placed = (P(None, "sp", "tp"), P(None, "sp", "tp"), P("tp"))
    return jax.shard_map(
        functools.partial(per_device, mesh.shape["sp"], mesh.shape["tp"]),
        mesh=mesh, in_specs=placed, out_specs=P(None, "sp", "tp"), check_vma=False,
    )
```

time: 505 us -> 24.2 us (0.05)
  the two profiles are of different devices: /device:TPU:0 before, /device:TPU:17 now
where the time goes in v1:
time: 24.2 us; the launch traced here: 24 us
  Pallas kernels  24 us (99%)
    pallas_call x1, Pallas kernels, per_device(): pl.pallas_call(functools.partial(scan_kernel, n, m, length, channels, wid...  21.8 us
    pallas_call x1, Pallas kernels, per_device(): pl.pallas_call(functools.partial(norm_kernel, rows), out_shape=jax.ShapeD...  2.22 us

profile of v1, /device:TPU:17, one launch (start us, length us, event | category | flops | bytes accessed | tf_op | source)
XLA Modules:
  0.0 24.0 jit_solution(13921838385649444495)
XLA Ops:
  0.0 0.0 copy-start
  0.0 21.8 %scan.1 = (f32[8,1024,256]{2,1,0:T(8,128)S(1)}, f32[1024,128]{1,0:T(8,128)S(1)}) custom-call(f32[1,1024,2048]{2,1,0:T(8,128)} %fade_hbm.1, bf16[1,1024,2048]{2,1,0:T(8,128)(2,1)} %update_hbm.1), custom_call_target="tpu_custom_call" | custom-call | tf_op jit(solution)/shard_map/scan/pallas_call | solution.py:210
  21.8 0.0 copy-done
  21.8 2.2 %norm.1 = bf16[1,1024,2048]{2,1,0:T(8,128)(2,1)} custom-call(f32[8,1024,256]{2,1,0:T(8,128)S(1)} %get-tuple-element.7.state_ref, f32[1024,128]{1,0:T(8,128)S(1)} %get-tuple-element.8.gain_ref, f32[1,2048]{1,0:T(1,128)S(1)} %bitcast.1), custom_call_target="tpu_custom_call" | custom-call | tf_op jit(solution)/shard_map/norm/pallas_call | solution.py:239
Async XLA Ops:
  0.0 21.8 %copy-start = (f32[2048]{0:T(1024)S(1)}, f32[2048]{0:T(1024)}, u32[]{:S(2)}) copy-start(f32[2048]{0:T(1024)} %param.5) | copy-start | bytes 24580

commit v2 on v1

v2 whole, which is shorter than its diff:
```python
import functools

import jax
import jax.numpy as jnp
from jax import lax
from jax.experimental import pallas as pl
from jax.experimental.pallas import tpu as pltpu
from jax.sharding import PartitionSpec as P

MESH = pl.DeviceIdType.MESH
EPS = 1e-06
AHEAD = 4
BROAD = 1024
SLICE = 256


def piece_of(size, most):
    most = min(size, most)
    while size % most:
        most //= 2
    return most


def group_of(n):
    group = 1
    while group * group < n:
        group *= 2
    return group


def scan_kernel(
    n, m, length, wide, rows, group,
    fade_hbm, update_hbm, state_ref, square_ref,
    fade_buf, update_buf, fall_buf, tri, ends, summary, near, passed, far, squares, got_squares,
    fade_sem, update_sem, near_send, near_recv, far_send, far_recv, sq_send_sem, sq_recv_sem,
):
    me, part = lax.axis_index("sp"), lax.axis_index("tp")
    blocks, span, _ = state_ref.shape
    pieces = span // rows
    lots, _, broad = fade_buf.shape
    strips, times = broad // wide, fade_sem.shape[0] // lots
    tall = span // times
    bunches = n // group
    bunch, rank = me // group, lax.rem(me, group)

    def fetch(i):
        lot, time = i // times, lax.rem(i, times)
        here = pl.ds(pl.multiple_of(time * tall, tall), tall)
        columns = pl.ds(pl.multiple_of(lot * broad, broad), broad)
        return (
            pltpu.make_async_copy(
                fade_hbm.at[0, here, columns], fade_buf.at[lot, here, :], fade_sem.at[i]
            ),
            pltpu.make_async_copy(
                update_hbm.at[0, here, columns], update_buf.at[lot, here, :], update_sem.at[i]
            ),
        )

    ahead = min(AHEAD, lots * times)
    for i in range(ahead):
        for copy in fetch(jnp.int32(i)):
            copy.start()

    barrier = pltpu.get_barrier_semaphore()
    for step in range(1, group):
        other = bunch * group + lax.rem(rank + step, group)
        pl.semaphore_signal(barrier, inc=1, device_id=(other, part), device_id_type=MESH)
    for step in range(1, bunches):
        other = lax.rem(me + step * group, n)
        pl.semaphore_signal(barrier, inc=1, device_id=(other, part), device_id_type=MESH)
    for step in range(1, m):
        other = lax.rem(part + step, m)
        pl.semaphore_signal(barrier, inc=1, device_id=(me, other), device_id_type=MESH)

    later = lax.broadcasted_iota(jnp.int32, (rows, 2 * rows), 0)
    sooner = lax.rem(lax.broadcasted_iota(jnp.int32, (rows, 2 * rows), 1), rows)
    tri[...] = jnp.where(sooner <= later, 1.0, 0.0).astype(jnp.bfloat16)

    def tell_near(b, step):
        other = bunch * group + lax.rem(rank + step, group)
        return pltpu.make_async_remote_copy(
            src_ref=summary.at[b],
            dst_ref=near.at[b, step - 1],
            send_sem=near_send.at[b, step - 1],
            recv_sem=near_recv.at[b, step - 1],
            device_id=(other, part),
            device_id_type=MESH,
        )

    def tell_far(b, other):
        return pltpu.make_async_remote_copy(
            src_ref=passed.at[b],
            dst_ref=far.at[b, bunch],
            send_sem=far_send.at[b, other],
            recv_sem=far_recv.at[b, bunch],
            device_id=(other * group + rank, part),
            device_id_type=MESH,
        )

    def hear_far(b, other):
        return pltpu.make_async_remote_copy(
            src_ref=passed.at[b],
            dst_ref=far.at[b, other],
            send_sem=far_send.at[b, other],
            recv_sem=far_recv.at[b, other],
            device_id=(lax.rem(me + group, n), part),
            device_id_type=MESH,
        )

    def dot(a, b):
        return jnp.dot(a, b, preferred_element_type=jnp.float32)

    rate = 1.4426950408889634 / length

    summary[:, 0:1, :] = jnp.ones((lots, 1, broad), jnp.float32)
    summary[:, 1:2, :] = jnp.zeros((lots, 1, broad), jnp.float32)

    @pl.loop(0, lots * times)
    def _(i):
        for copy in fetch(i):
            copy.wait()

        @pl.when(i + ahead < lots * times)
        def _():
            for copy in fetch(i + ahead):
                copy.start()

        lot, time = i // times, lax.rem(i, times)
        for strip in range(strips):
            mine = slice(strip * wide, (strip + 1) * wide)
            b = lot * strips + strip
            total_fall, total = summary[lot, 0:1, mine], summary[lot, 1:2, mine]
            for k in range(tall // rows):
                here = pl.ds(pl.multiple_of(time * tall + k * rows, rows), rows)
                fade = fade_buf[lot, here, mine]
                faded = dot(tri[:, :rows], fade.astype(jnp.bfloat16)) * rate
                last_fall = jnp.exp2(jnp.sum(fade, axis=0, keepdims=True) * -rate)
                push = update_buf[lot, here, mine]
                extra = push.astype(jnp.float32) * (jnp.exp2(faded) - 1.0)
                both = jnp.concatenate([push, extra.astype(jnp.bfloat16)], axis=0)
                grown = dot(tri[...], both)
                fall_buf[b, here, :] = jnp.exp2(-faded)
                state_ref[b, here, :] = grown
                ends[b, time * (tall // rows) + k, :, :] = last_fall
                total = last_fall * (grown[rows - 1 : rows, :] + total)
                total_fall = total_fall * last_fall
            summary[lot, 0:1, mine] = total_fall
            summary[lot, 1:2, mine] = total

        @pl.when(i == times - 1)
        def _():
            pl.semaphore_wait(barrier, group + bunches + m - 3)

        @pl.when(time == times - 1)
        def _():
            for step in range(1, group):
                tell_near(lot, step).start()

    @pl.loop(0, lots)
    def _(b):
        for step in range(1, group):
            tell_near(b, step).wait_recv()

        fall = jnp.ones((1, broad), jnp.float32)
        value = jnp.zeros((1, broad), jnp.float32)
        for place in range(group):
            one_fall, one = summary[b, 0:1, :], summary[b, 1:2, :]
            for step in range(1, group):
                came = lax.rem(rank - place + group, group) == step
                one_fall = jnp.where(came, near[b, step - 1, 0:1, :], one_fall)
                one = jnp.where(came, near[b, step - 1, 1:2, :], one)
            fall = fall * one_fall
            value = one_fall * value + one
        passed[b, 0:1, :] = fall
        passed[b, 1:2, :] = value

        @pl.loop(bunch + 1, bunches)
        def _(other):
            tell_far(b, other).start()

    def share(k, step):
        other = lax.rem(part + step, m)
        return pltpu.make_async_remote_copy(
            src_ref=squares.at[k],
            dst_ref=got_squares.at[step - 1, k],
            send_sem=sq_send_sem.at[step - 1, k],
            recv_sem=sq_recv_sem.at[step - 1, k],
            device_id=(me, other),
            device_id_type=MESH,
        )

    squares[...] = jnp.zeros_like(squares)

    @pl.loop(0, lots)
    def _(lot):
        def take(other, entering):
            hear_far(lot, other).wait_recv()
            return far[lot, other, 0:1, :] * entering + far[lot, other, 1:2, :]

        entering = lax.fori_loop(0, bunch, take, jnp.zeros((1, broad), jnp.float32))
        for place in range(group - 1):
            one_fall, one = near[lot, 0, 0:1, :], near[lot, 0, 1:2, :]
            for step in range(2, group):
                came = rank - place == step
                one_fall = jnp.where(came, near[lot, step - 1, 0:1, :], one_fall)
                one = jnp.where(came, near[lot, step - 1, 1:2, :], one)
            before = place < rank
            entering = jnp.where(before, one_fall * entering + one, entering)
        starts = [entering[:, t * wide : (t + 1) * wide] for t in range(strips)]

        def finish(k, starts):
            here = pl.ds(pl.multiple_of(k * rows, rows), rows)
            square = squares[k]
            leaving = []
            for strip in range(strips):
                b = lot * strips + strip
                grown = state_ref[b, here, :] + starts[strip]
                state = fall_buf[b, here, :] * grown
                state_ref[b, here, :] = state
                leaving.append(ends[b, k, :, :] * grown[rows - 1 : rows, :])
                for c in range(wide // 128):
                    part_state = state[:, c * 128 : (c + 1) * 128]
                    square = square + part_state * part_state
            squares[k] = square

            @pl.when(lot == lots - 1)
            def _():
                for step in range(1, m):
                    share(k, step).start()

            return tuple(leaving)

        lax.fori_loop(0, pieces, finish, tuple(starts))

    @pl.loop(0, pieces)
    def _(k):
        square = squares[k]
        for step in range(1, m):
            share(k, step).wait_recv()
            square = square + got_squares[step - 1, k]
        square_ref[pl.ds(pl.multiple_of(k * rows, rows), rows), :] = square
        for step in range(1, m):
            share(k, step).wait_send()

    @pl.loop(0, lots)
    def _(b):
        for step in range(1, group):
            tell_near(b, step).wait_send()

        @pl.loop(bunch + 1, bunches)
        def _(other):
            tell_far(b, other).wait_send()


def norm_kernel(length, channels, rows, state_ref, square_ref, norm_gain_ref, out_hbm, out_buf, sem):
    blocks, span, wide = state_ref.shape
    pieces = span // rows

    def put(k):
        here = pl.ds(pl.multiple_of(k * rows, rows), rows)
        return pltpu.make_async_copy(out_buf.at[k], out_hbm.at[0, here, :], sem.at[k])

    @pl.loop(0, pieces)
    def _(k):
        here = pl.ds(pl.multiple_of(k * rows, rows), rows)
        power = jnp.sum(square_ref[here, :], axis=1, keepdims=True) / (length * channels)
        gain = jnp.broadcast_to(lax.rsqrt(power + EPS) * length ** (-0.5), (rows, 128))
        for b in range(blocks):
            for c in range(wide // 128):
                columns = pl.ds(b * wide + c * 128, 128)
                state = state_ref[b, here, pl.ds(c * 128, 128)]
                out_buf[k, :, columns] = (state * gain * norm_gain_ref[:, columns]).astype(
                    out_buf.dtype
                )
        put(k).start()

    @pl.loop(0, pieces)
    def _(k):
        put(k).wait()


def per_device(n, m, fade_rate, update_in, norm_gain):
    _, span, own = fade_rate.shape
    length, channels = span * n, own * m
    wide, rows = piece_of(own, 256), piece_of(span, 128)
    group = group_of(n)
    broad, tall = piece_of(own, BROAD), piece_of(span, SLICE)
    lots, times = own // broad, span // tall
    blocks, pieces = own // wide, span // rows
    f32, bf16 = jnp.float32, jnp.bfloat16
    anywhere = pl.BlockSpec(memory_space=pl.ANY)
    in_vmem = pl.BlockSpec(memory_space=pltpu.VMEM)
    dma = pltpu.SemaphoreType.DMA
    state, square = pl.pallas_call(
        functools.partial(scan_kernel, n, m, length, wide, rows, group),
        out_shape=(
            pltpu.VMEM((blocks, span, wide), f32),
            pltpu.VMEM((span, 128), f32),
        ),
        in_specs=[anywhere, anywhere],
        out_specs=(in_vmem, in_vmem),
        scratch_shapes=[
            pltpu.VMEM((lots, span, broad), f32),
            pltpu.VMEM((lots, span, broad), bf16),
            pltpu.VMEM((blocks, span, wide), f32),
            pltpu.VMEM((rows, 2 * rows), bf16),
            pltpu.VMEM((blocks, pieces, 1, wide), f32),
            pltpu.VMEM((lots, 2, broad), f32),
            pltpu.VMEM((lots, group - 1, 2, broad), f32),
            pltpu.VMEM((lots, 2, broad), f32),
            pltpu.VMEM((lots, n // group, 2, broad), f32),
            pltpu.VMEM((pieces, rows, 128), f32),
            pltpu.VMEM((m - 1, pieces, rows, 128), f32),
            dma((lots * times,)),
            dma((lots * times,)),
            dma((lots, group - 1)),
            dma((lots, group - 1)),
            dma((lots, n // group)),
            dma((lots, n // group)),
            dma((m - 1, pieces)),
            dma((m - 1, pieces)),
        ],
        compiler_params=pltpu.CompilerParams(
            collective_id=0, has_side_effects=True, vmem_limit_bytes=44 * 2**20
        ),
        name="scan",
    )(fade_rate, update_in)
    return pl.pallas_call(
        functools.partial(norm_kernel, length, channels, rows),
        out_shape=jax.ShapeDtypeStruct((1, span, own), bf16),
        in_specs=[in_vmem, in_vmem, in_vmem],
        out_specs=anywhere,
        scratch_shapes=[pltpu.VMEM((pieces, rows, own), bf16), dma((pieces,))],
        compiler_params=pltpu.CompilerParams(vmem_limit_bytes=24 * 2**20),
        name="norm",
    )(state, square, norm_gain.reshape(1, own))


def solution(mesh):
    placed = (P(None, "sp", "tp"), P(None, "sp", "tp"), P("tp"))
    return jax.shard_map(
        functools.partial(per_device, mesh.shape["sp"], mesh.shape["tp"]),
        mesh=mesh, in_specs=placed, out_specs=P(None, "sp", "tp"), check_vma=False,
    )
```

time: 24.2 us -> 18 us (0.74)
  Pallas kernels: 24 us -> 17.9 us
    pallas_call x2, Pallas kernels: 24 us -> 17.9 us  [the longest x1 15.3 us: per_device(): pl.pallas_call(functools.partial(scan_kernel, n, m, length, wide, rows, g...]
where the time goes in v2:
time: 18 us; the launch traced here: 17.9 us
  Pallas kernels  17.9 us (99%)
    pallas_call x1, Pallas kernels, per_device(): pl.pallas_call(functools.partial(scan_kernel, n, m, length, wide, rows, g...  15.3 us
    pallas_call x1, Pallas kernels, per_device(): pl.pallas_call(functools.partial(norm_kernel, length, channels, rows), ou...  2.54 us

profile of v2, /device:TPU:17, one launch (start us, length us, event | category | flops | bytes accessed | tf_op | source)
XLA Modules:
  0.0 17.9 jit_solution(10290139917672691602)
XLA Ops:
  0.0 0.0 copy-start
  0.0 15.3 %scan.1 = (f32[8,1024,256]{2,1,0:T(8,128)S(1)}, f32[1024,128]{1,0:T(8,128)S(1)}) custom-call(f32[1,1024,2048]{2,1,0:T(8,128)} %fade_hbm.1, bf16[1,1024,2048]{2,1,0:T(8,128)(2,1)} %update_hbm.1), custom_call_target="tpu_custom_call" | custom-call | tf_op jit(solution)/shard_map/scan/pallas_call | solution.py:294
  15.4 0.0 copy-done
  15.4 2.5 %norm.1 = bf16[1,1024,2048]{2,1,0:T(8,128)(2,1)} custom-call(f32[8,1024,256]{2,1,0:T(8,128)S(1)} %get-tuple-element.7.state_ref, f32[1024,128]{1,0:T(8,128)S(1)} %get-tuple-element.8.square_ref, f32[1,2048]{1,0:T(1,128)S(1)} %bitcast.1), custom_call_target="tpu_custom_call" | custom-call | tf_op jit(solution)/shard_map/norm/pallas_call | solution.py:328
Async XLA Ops:
  0.0 15.4 %copy-start = (f32[2048]{0:T(1024)S(1)}, f32[2048]{0:T(1024)}, u32[]{:S(2)}) copy-start(f32[2048]{0:T(1024)} %param.5) | copy-start | bytes 24580

commit v3 on v2

--- a/solution.py
+++ b/solution.py
@@ -9,7 +9,7 @@
 
 MESH = pl.DeviceIdType.MESH
 EPS = 1e-06
-AHEAD = 4
+AHEAD = 8
 BROAD = 1024
 SLICE = 256
 

time: 18 us -> 18 us (level)
  no operation moved by 1% of the time
where the time goes in v3:
time: 18 us; the launch traced here: 17.9 us
  Pallas kernels  17.9 us (99%)
    pallas_call x1, Pallas kernels, per_device(): pl.pallas_call(functools.partial(scan_kernel, n, m, length, wide, rows, g...  15.3 us
    pallas_call x1, Pallas kernels, per_device(): pl.pallas_call(functools.partial(norm_kernel, length, channels, rows), ou...  2.54 us

profile of v3, /device:TPU:17, one launch (start us, length us, event | category | flops | bytes accessed | tf_op | source)
XLA Modules:
  0.0 17.9 jit_solution(6437857707188017072)
XLA Ops:
  0.0 0.0 copy-start
  0.0 15.3 %scan.1 = (f32[8,1024,256]{2,1,0:T(8,128)S(1)}, f32[1024,128]{1,0:T(8,128)S(1)}) custom-call(f32[1,1024,2048]{2,1,0:T(8,128)} %fade_hbm.1, bf16[1,1024,2048]{2,1,0:T(8,128)(2,1)} %update_hbm.1), custom_call_target="tpu_custom_call" | custom-call | tf_op jit(solution)/shard_map/scan/pallas_call | solution.py:294
  15.3 0.0 copy-done
  15.4 2.5 %norm.1 = bf16[1,1024,2048]{2,1,0:T(8,128)(2,1)} custom-call(f32[8,1024,256]{2,1,0:T(8,128)S(1)} %get-tuple-element.7.state_ref, f32[1024,128]{1,0:T(8,128)S(1)} %get-tuple-element.8.square_ref, f32[1,2048]{1,0:T(1,128)S(1)} %bitcast.1), custom_call_target="tpu_custom_call" | custom-call | tf_op jit(solution)/shard_map/norm/pallas_call | solution.py:328
Async XLA Ops:
  0.0 15.3 %copy-start = (f32[2048]{0:T(1024)S(1)}, f32[2048]{0:T(1024)}, u32[]{:S(2)}) copy-start(f32[2048]{0:T(1024)} %param.5) | copy-start | bytes 24580
